TPU v7x, 32 devices: a whole 2x2x4 slice. The times are simulated.
32 devices in a mesh: seq: 4 (over y, core), fsdp: 8 (over z, x).
Axes of the slice: x: 2, y: 2, z: 4, core: 2. Of those that a mesh axis runs over, the one named last changes fastest.
Arguments:
- tokens: bfloat16 [8, 1536, 1024], P('fsdp', 'seq'), may hold values from -6 to 6
- lengths: int32 [8, 3], P('fsdp'), may hold values from 1 to 1024, 1536 in all within a row
- time_steps: int32 [8, 3], P('fsdp'), may hold values from 0 to 999
- order: int32 [8, 1536], P('fsdp', 'seq'), may hold values from 0 to 1535, each once within a row
- w_time: bfloat16 [256, 2048], P('fsdp'), may hold values from -0.375 to 0.375
- w_qkv: bfloat16 [1024, 3072], P('fsdp'), may hold values from -0.1875 to 0.1875
- w_out: bfloat16 [1024, 1024], P('fsdp'), may hold values from -1.5 to 1.5
- w_up: bfloat16 [1024, 4096], P('fsdp'), may hold values from -0.1875 to 0.1875
- w_down: bfloat16 [4096, 1024], P('fsdp'), may hold values from -0.09375 to 0.09375
- cotangent: bfloat16 [8, 1536, 1024], P('fsdp', 'seq'), may hold values from -6 to 6
Outputs:
- output: bfloat16 [8, 1536, 1024], P('fsdp', 'seq')
- input_grad: float32 [8, 1536, 1024], P('fsdp', 'seq')
- grad_time: float32 [256, 2048], P('fsdp')
- grad_qkv: float32 [1024, 3072], P('fsdp')
- grad_out: float32 [1024, 1024], P('fsdp')
- grad_up: float32 [1024, 4096], P('fsdp')
- grad_down: float32 [4096, 1024], P('fsdp')
Inputs may be any that keep to these rules, and one draw needn't show every extreme that they name: Each group's 3 lengths sum to 1536; the longest is exactly 1024. `order`: each group's row is a permutation of the indices 0 to 1535.
All inputs are finite; a program needn't handle non-finite values.
Results may differ from a plain program's by a relative error of at most 0.02.
Values may be sent and summed in bfloat16 or wider, within the bound.
A program may use at most 192 MiB of HBM per device.

v0:
```python
import math
import jax
import jax.numpy as jnp
from jax import lax
from jax.sharding import PartitionSpec as P

D = 1024
H = 16
HD = 64
TEMB = 256
NSEQ = 3
EPS = 1e-05
NEG = -1e30
BASE = 10000.0
BLOCK_ROWS = 512


def time_embedding(steps):
    half = TEMB // 2
    freqs = jnp.exp(-math.log(BASE) * jnp.arange(half, dtype=jnp.float32) / half)
    angles = steps.astype(jnp.float32)[:, None] * freqs[None, :]
    return jnp.concatenate([jnp.sin(angles), jnp.cos(angles)], axis=-1)


def layout(lens, places):
    ends = jnp.cumsum(lens)
    starts = ends - lens
    member = (places[:, None] >= starts[None, :]) & (places[:, None] < ends[None, :])
    labels = jnp.arange(NSEQ, dtype=jnp.int32)
    segment = jnp.sum(jnp.where(member, labels[None, :], 0), axis=1)
    offset = places - jnp.sum(jnp.where(member, starts[None, :], 0), axis=1)
    return (member.astype(jnp.float32), segment, offset)


def rotate(values, offset, sign):
    half = HD // 2
    freqs = jnp.exp(-math.log(BASE) * jnp.arange(half, dtype=jnp.float32) * 2.0 / HD)
    angles = offset.astype(jnp.float32)[:, None] * freqs[None, :]
    cosine = jnp.cos(angles)[:, None, :]
    sine = sign * jnp.sin(angles)[:, None, :]
    first = values[..., :half]
    second = values[..., half:]
    return jnp.concatenate(
        [first * cosine - second * sine, second * cosine + first * sine], axis=-1
    )


def norm_mod(values, scale):
    centre = jnp.mean(values, axis=-1, keepdims=True)
    centred = values - centre
    spread = jnp.mean(centred * centred, axis=-1, keepdims=True)
    return centred * lax.rsqrt(spread + EPS) * (1.0 + scale)


def contract_rows(left, right):
    return lax.dot_general(
        left, right, (((0,), (0,)), ((), ())), preferred_element_type=jnp.float32
    )


def contract_cols(left, right):
    return lax.dot_general(
        left, right, (((1,), (1,)), ((), ())), preferred_element_type=jnp.float32
    )


def weight_rows(left, weight):
    return (
        jnp.dot(
            left,
            lax.all_gather(weight, "fsdp", axis=0, tiled=True),
            preferred_element_type=jnp.float32,
        ),
        weight,
    )


def weight_cols(grad, weight):
    return contract_cols(grad, lax.all_gather(weight, "fsdp", axis=0, tiled=True))


def weight_grad(left, grad):

    def term():
        if grad.dtype == jnp.float32:
            return lax.dot_general(
                left.astype(jnp.float32),
                grad,
                (((0,), (0,)), ((), ())),
                precision=lax.Precision.HIGHEST,
                preferred_element_type=jnp.float32,
            )
        return contract_rows(left, grad)

    shard = lax.psum_scatter(
        term().astype(jnp.bfloat16), "fsdp", scatter_dimension=0, tiled=True
    ).astype(jnp.float32)
    shard = lax.psum(shard.astype(jnp.bfloat16), "seq").astype(jnp.float32)
    return shard


def to_heads(packed):
    return lax.all_to_all(packed, "seq", split_axis=2, concat_axis=0, tiled=True)


def to_rows(packed):
    return lax.all_to_all(packed, "seq", split_axis=0, concat_axis=2, tiled=True)


def reorder(data, wanted, labels):
    pick = (wanted[:, None] == labels[None, :]).astype(jnp.bfloat16)
    return jnp.dot(
        pick, lax.all_gather(data, "seq", axis=0, tiled=True), preferred_element_type=jnp.float32
    )


def slice_cols(matrix, start):
    return lax.dynamic_slice_in_dim(matrix, start, HD, 1)


def head_forward(query, key, value, segment, block):
    group = query.shape[0]
    factor = HD ** (-0.5)

    def one_block(index):
        start = index * block
        q_blk = lax.dynamic_slice_in_dim(query, start, block, 0)
        s_blk = lax.dynamic_slice_in_dim(segment, start, block, 0)
        scores = contract_cols(q_blk, key) * factor
        scores = jnp.where(s_blk[:, None] == segment[None, :], scores, NEG)
        peak = jnp.max(scores, axis=1, keepdims=True)
        expo = jnp.exp(scores - peak)
        total = jnp.sum(expo, axis=1, keepdims=True)
        probs = (expo / total).astype(jnp.bfloat16)
        mixed = jnp.dot(probs, value, preferred_element_type=jnp.float32)
        return (mixed.astype(jnp.bfloat16), (peak + jnp.log(total))[:, 0])

    mixed, logsum = lax.map(one_block, jnp.arange(group // block))
    return (mixed.reshape(group, HD), logsum.reshape(group))


def head_backward(query, key, value, logsum, d_mixed, segment, offset, block):
    group = query.shape[0]
    factor = HD ** (-0.5)

    def step(carry, index):
        d_key, d_value = carry
        start = index * block
        q_blk = lax.dynamic_slice_in_dim(query, start, block, 0)
        s_blk = lax.dynamic_slice_in_dim(segment, start, block, 0)
        l_blk = lax.dynamic_slice_in_dim(logsum, start, block, 0)
        g_blk = lax.dynamic_slice_in_dim(d_mixed, start, block, 0)
        scores = contract_cols(q_blk, key) * factor
        probs = jnp.where(s_blk[:, None] == segment[None, :], jnp.exp(scores - l_blk[:, None]), 0.0)
        probs_low = probs.astype(jnp.bfloat16)
        d_value = d_value + contract_rows(probs_low, g_blk)
        d_probs = contract_cols(g_blk, value)
        delta = jnp.sum(probs * d_probs, axis=1, keepdims=True)
        d_scores = (probs * (d_probs - delta)).astype(jnp.bfloat16)
        d_query = jnp.dot(d_scores, key, preferred_element_type=jnp.float32) * factor
        d_key = d_key + contract_rows(d_scores, q_blk) * factor
        return ((d_key, d_value), d_query)

    zeros = jnp.zeros((group, HD), jnp.float32)
    (d_key, d_value), d_query = lax.scan(step, (zeros, zeros), jnp.arange(group // block))
    d_query = d_query.reshape(group, HD)
    back_query = rotate(d_query[:, None, :], offset, -1.0)[:, 0, :]
    back_key = rotate(d_key[:, None, :], offset, -1.0)[:, 0, :]
    return (back_query, back_key, d_value)


def on_device(tokens, lengths, time_steps, order, w_time, w_qkv, w_out, w_up, w_down, cotangent):
    rows = tokens.shape[1]
    slices = lax.axis_size("seq")
    local_heads = H // slices
    group = rows * slices
    block = min(BLOCK_ROWS, group)
    lens = lengths[0]
    places = order[0]
    order_all = lax.all_gather(places, "seq", axis=0, tiled=True)
    member_mine, segment_mine, offset_mine = layout(lens, places)
    member_all, segment_all, offset_all = layout(lens, order_all)
    emb = time_embedding(time_steps[0]).astype(jnp.bfloat16)
    scales_seq, whole_time = weight_rows(emb, w_time)
    scales = jnp.dot(member_mine, scales_seq, precision=lax.Precision.HIGHEST)
    scale_one = scales[:, :D]
    scale_two = scales[:, D:]
    inputs = tokens[0].astype(jnp.float32)
    normed_one, pull_one = jax.vjp(norm_mod, inputs, scale_one)
    h_one = normed_one.astype(jnp.bfloat16)
    projected, whole_qkv = weight_rows(h_one, w_qkv)
    query = rotate(projected[:, :D].reshape(rows, H, HD), offset_mine, 1.0).reshape(rows, D)
    key = rotate(projected[:, D : 2 * D].reshape(rows, H, HD), offset_mine, 1.0).reshape(rows, D)
    packed = jnp.stack([query, key, projected[:, 2 * D :]], axis=1).astype(jnp.bfloat16)
    heads_qkv = to_heads(packed.reshape(rows, 3, slices, local_heads * HD))
    q_heads = heads_qkv[:, 0, 0]
    k_heads = heads_qkv[:, 1, 0]
    v_heads = heads_qkv[:, 2, 0]

    def forward_head(index):
        start = index * HD
        return head_forward(
            slice_cols(q_heads, start),
            slice_cols(k_heads, start),
            slice_cols(v_heads, start),
            segment_all,
            block,
        )

    mixed_heads, logsum_heads = lax.map(forward_head, jnp.arange(local_heads))
    mixed_cat = mixed_heads.transpose(1, 0, 2).reshape(group, 1, 1, local_heads * HD)
    mixed = to_rows(mixed_cat).reshape(rows, D)
    attn_out, whole_out = weight_rows(mixed, w_out)
    x_two = inputs + attn_out
    normed_two, pull_two = jax.vjp(norm_mod, x_two, scale_two)
    h_two = normed_two.astype(jnp.bfloat16)
    up, whole_up = weight_rows(h_two, w_up)
    activated, pull_gelu = jax.vjp(jax.nn.gelu, up)
    hidden = activated.astype(jnp.bfloat16)
    ffn_out, whole_down = weight_rows(hidden, w_down)
    result = (x_two + ffn_out).astype(jnp.bfloat16)
    mine = lax.axis_index("seq") * rows + jnp.arange(rows, dtype=jnp.int32)
    output = reorder(result, mine, order_all).astype(jnp.bfloat16)
    every = jnp.arange(group, dtype=jnp.int32)
    d_result = reorder(cotangent[0], places, every)
    d_low = d_result.astype(jnp.bfloat16)
    d_hidden = weight_cols(d_low, w_down)
    grad_down = weight_grad(hidden, d_low)
    d_up = pull_gelu(d_hidden)[0].astype(jnp.bfloat16)
    grad_up = weight_grad(h_two, d_up)
    d_htwo = weight_cols(d_up, w_up)
    d_xpart, d_scale_two = pull_two(d_htwo)
    d_xtwo = d_result + d_xpart
    d_attn = d_xtwo.astype(jnp.bfloat16)
    grad_out = weight_grad(mixed, d_attn)
    d_mixed = weight_cols(d_attn, w_out).astype(jnp.bfloat16)
    d_heads = to_heads(d_mixed.reshape(rows, 1, slices, local_heads * HD))[:, 0, 0]

    def backward_head(index):
        start = index * HD
        return head_backward(
            slice_cols(q_heads, start),
            slice_cols(k_heads, start),
            slice_cols(v_heads, start),
            logsum_heads[index],
            slice_cols(d_heads, start),
            segment_all,
            offset_all,
            block,
        )

    d_query, d_key, d_value = lax.map(backward_head, jnp.arange(local_heads))
    stacked = jnp.stack([d_query, d_key, d_value], axis=1)
    stacked = (
        stacked.transpose(2, 1, 0, 3).reshape(group, 3, 1, local_heads * HD).astype(jnp.bfloat16)
    )
    d_qkv = to_rows(stacked).reshape(rows, 3 * D)
    grad_qkv = weight_grad(h_one, d_qkv)
    d_hone = weight_cols(d_qkv, w_qkv)
    d_xone, d_scale_one = pull_one(d_hone)
    input_grad = d_xtwo + d_xone
    d_scales = lax.dot_general(
        member_mine,
        jnp.concatenate([d_scale_one, d_scale_two], axis=1),
        (((0,), (0,)), ((), ())),
        precision=lax.Precision.HIGHEST,
        preferred_element_type=jnp.float32,
    )
    grad_time = weight_grad(emb, d_scales)
    grads = (grad_time, grad_qkv, grad_out, grad_up, grad_down)
    return (output[None], input_grad[None], grads[0], grads[1], grads[2], grads[3], grads[4])


def solution(mesh):
    return jax.shard_map(
        on_device,
        mesh=mesh,
        in_specs=(
            P("fsdp", "seq", None),
            P("fsdp", None),
            P("fsdp", None),
            P("fsdp", "seq"),
            P("fsdp", None),
            P("fsdp", None),
            P("fsdp", None),
            P("fsdp", None),
            P("fsdp", None),
            P("fsdp", "seq", None),
        ),
        out_specs=(
            P("fsdp", "seq", None),
            P("fsdp", "seq", None),
            P("fsdp", None),
            P("fsdp", None),
            P("fsdp", None),
            P("fsdp", None),
            P("fsdp", None),
        ),
        check_vma=False,
    )
```

profile of v0, /device:TPU:0, one launch (start us, length us, event | category | flops | bytes accessed | tf_op | source)
XLA Modules:
  0.0 1447.6 jit_solution(13211309296788337764)
XLA Ops:
  11.9 41.2 %all-gather.10.cloned.1.call-done = bf16[256,2048]{1,0:T(8,128)(2,1)} async-done(((bf16[32,2048]{1,0:T(8,128)(2,1)}), bf16[256,2048]{1,0:T(8,128)(2,1)}) %all-gather.10.cloned.1.call-update) | async-done | bytes 1048592 | tf_op jit(solution)/shard_map/all_gather | solution.py:71
  58.2 94.6 %all-gather.12.cloned.1.call-done = bf16[1024,3072]{1,0:T(8,128)(2,1)} async-done(((bf16[128,3072]{1,0:T(8,128)(2,1)}), bf16[1024,3072]{1,0:T(8,128)(2,1)}) %all-gather.12.cloned.1.call-update) | async-done | bytes 6291472 | tf_op jit(solution)/shard_map/all_gather | solution.py:71
  152.8 4.7 fusion.97
  160.9 3.4 fusion.95
  170.3 3.6 all-to-all-start
  174.5 31.2 %all-gather = s32[1,1536]{1,0:T(1,128)S(1)} all-gather(s32[1,384]{1,0:T(1,128)S(1)} %copy-done.57), channel_id=2, replica_groups=mesh['seq'=4,'fsdp'=8] {'seq'}, dimensions={1}, use_global_device_ids=true | all-gather | bytes 7680 | tf_op jit(solution)/shard_map/all_gather | solution.py:180
  209.0 2.9 slice_bitcast_fusion
  212.0 64.9 %while.88 = (s32[]{:T(128)}, bf16[4,1536,64]{1,2,0:T(8,128)(2,1)S(1)}, f32[4,1536]{1,0:T(4,128)}, s32[4]{0:T(128)S(1)}, bf16[1536,256]{1,0:T(8,128)(2,1)}, /*ind...) while((s32[]{:T(128)}, ...), condition=%wide.region_10.11_spmd, body=%wide.region_5.0_spmd.sunk | while | flops 208436736 | bytes 12839458 | solution.py:210
  215.7 10.6 while.91
  231.9 10.6 while.91
  248.2 10.6 while.91
  264.4 10.6 while.91
  279.9 3.7 all-to-all-start.1
  283.6 4.5 fusion.49
  288.1 7.1 all-to-all-done.1
  297.2 3.2 fusion.96
  302.8 59.8 %all-gather.16.cloned.1.call-done = bf16[1024,4096]{1,0:T(8,128)(2,1)} async-done(((bf16[128,4096]{1,0:T(8,128)(2,1)}), bf16[1024,4096]{1,0:T(8,128)(2,1)}) %all-gather.16.cloned.1.call-update) | async-done | bytes 8388624 | tf_op jit(solution)/shard_map/all_gather | solution.py:71
  362.6 9.9 fusion.98
  372.5 114.8 %all-gather.18.cloned.1.call-done = bf16[4096,1024]{1,0:T(8,128)(2,1)} async-done(((bf16[512,1024]{1,0:T(8,128)(2,1)}), bf16[4096,1024]{1,0:T(8,128)(2,1)}) %all-gather.18.cloned.1.call-update) | async-done | bytes 8388624 | tf_op jit(solution)/shard_map/all_gather | solution.py:71
  487.2 10.7 fusion.44
  498.0 3.8 multiply_reduce_fusion.1
  510.1 3.5 all-to-all-start.2
  517.0 8.2 all-to-all-done.2
  525.7 255.7 %while.90 = (s32[]{:T(128)}, bf16[4,1536,64]{1,2,0:T(8,128)(2,1)}, bf16[4,1536,64]{1,2,0:T(8,128)(2,1)}, bf16[4,1536,64]{1,2,0:T(8,128)(2,1)}, s32[4]{0:T(128)},...) while((s32[]{:T(128)}, bf16[4,1536,64]{1,2,0:T(8,128)(2,1)}, ...), condition=%wide.region_20.21_spmd, body=%wide.region_16.20_spmd.sunk | while | flops 513375776 | bytes 57267424 | solution.py:252
  535.7 48.1 %while.92 = (s32[]{:T(128)}, f32[1536,64]{0,1:T(8,128)}, f32[1536,64]{0,1:T(8,128)}, f32[3,512,64]{1,0,2:T(4,128)}, s32[3]{0:T(128)}, /*index=5*/s32[1536]{0:T(1...) while((s32[]{:T(128)}, f32[1536,64]{0,1:T(8,128)}, ...), condition=%wide.region_19.19_spmd.clone, body=%wide.region_17.18_spmd.clone.sunk | while | flops 511704576 | bytes 37968256 | solution.py:165
  548.1 3.7 dynamic_update_slice.65
  559.0 2.8 fusion.159
  564.2 3.6 dynamic_update_slice.65
  575.1 2.8 fusion.159
  580.2 3.6 dynamic_update_slice.65
  599.7 48.1 %while.92 = (s32[]{:T(128)}, f32[1536,64]{0,1:T(8,128)}, f32[1536,64]{0,1:T(8,128)}, f32[3,512,64]{1,0,2:T(4,128)}, s32[3]{0:T(128)}, /*index=5*/s32[1536]{0:T(1...) while((s32[]{:T(128)}, f32[1536,64]{0,1:T(8,128)}, ...), condition=%wide.region_19.19_spmd.clone, body=%wide.region_17.18_spmd.clone.sunk | while | flops 511704576 | bytes 37968256 | solution.py:165
  612.0 3.6 dynamic_update_slice.65
  622.9 2.8 fusion.159
  628.1 3.6 dynamic_update_slice.65
  639.0 2.8 fusion.159
  644.1 3.6 dynamic_update_slice.65
  663.6 48.1 %while.92 = (s32[]{:T(128)}, f32[1536,64]{0,1:T(8,128)}, f32[1536,64]{0,1:T(8,128)}, f32[3,512,64]{1,0,2:T(4,128)}, s32[3]{0:T(128)}, /*index=5*/s32[1536]{0:T(1...) while((s32[]{:T(128)}, f32[1536,64]{0,1:T(8,128)}, ...), condition=%wide.region_19.19_spmd.clone, body=%wide.region_17.18_spmd.clone.sunk | while | flops 511704576 | bytes 37968256 | solution.py:165
  675.9 3.6 dynamic_update_slice.65
  686.8 2.8 fusion.159
  692.0 3.6 dynamic_update_slice.65
  702.9 2.8 fusion.159
  708.1 3.6 dynamic_update_slice.65
  727.5 48.1 %while.92 = (s32[]{:T(128)}, f32[1536,64]{0,1:T(8,128)}, f32[1536,64]{0,1:T(8,128)}, f32[3,512,64]{1,0,2:T(4,128)}, s32[3]{0:T(128)}, /*index=5*/s32[1536]{0:T(1...) while((s32[]{:T(128)}, f32[1536,64]{0,1:T(8,128)}, ...), condition=%wide.region_19.19_spmd.clone, body=%wide.region_17.18_spmd.clone.sunk | while | flops 511704576 | bytes 37968256 | solution.py:165
  739.8 3.6 dynamic_update_slice.65
  750.7 2.8 fusion.159
  755.9 3.6 dynamic_update_slice.65
  766.8 2.8 fusion.159
  771.9 3.6 dynamic_update_slice.65
  781.4 3.3 pad_maximum_fusion.1
  784.7 4.3 copy.79
  789.0 39.8 %all_to_all.63 = bf16[1536,3,1,256]{3,1,2,0:T(4,128)(2,1)S(1)} all-to-all(bf16[1536,3,1,256]{3,1,2,0:T(4,128)(2,1)S(1)} %copy.79), channel_id=1, replica_groups=mesh['seq'=4,'fsdp'=8] {'seq'}, dimensions={0} | all-to-all | bytes 4718592 | tf_op jit(solution)/shard_map/all_to_all | solution.py:107
  830.5 4.5 copy.81
  835.0 6.7 fusion.63
  846.9 5.6 convolution_convert_fusion.2
  853.6 8.6 convolution_convert_fusion.1
  863.6 10.8 convolution_convert_fusion
  875.8 10.1 add_convert_fusion
  886.0 22.6 %reduce-scatter.6.cloned.1.call-done = bf16[32,2048]{1,0:T(8,128)(2,1)} async-done(((bf16[256,2048]{1,0:T(8,128)(2,1)}), bf16[32,2048]{1,0:T(8,128)(2,1)}) %reduce-scatter.6.cloned.1.call-update) | async-done | bytes 131088 | tf_op jit(solution)/shard_map/reduce_scatter | solution.py:95
  908.6 120.7 %reduce-scatter.8.cloned.1.call-done = bf16[128,3072]{1,0:T(8,128)(2,1)} async-done(((bf16[1024,3072]{1,0:T(8,128)(2,1)}), bf16[128,3072]{1,0:T(8,128)(2,1)}) %reduce-scatter.8.cloned.1.call-update) | async-done | bytes 786448 | tf_op jit(solution)/shard_map/reduce_scatter | solution.py:95
  1029.3 150.2 %reduce-scatter.12.cloned.1.call-done = bf16[128,4096]{1,0:T(8,128)(2,1)} async-done(((bf16[1024,4096]{1,0:T(8,128)(2,1)}), bf16[128,4096]{1,0:T(8,128)(2,1)}) %reduce-scatter.12.cloned.1.call-update) | async-done | bytes 1048592 | tf_op jit(solution)/shard_map/reduce_scatter | solution.py:95
  1179.5 150.2 %reduce-scatter.14.cloned.1.call-done = bf16[512,1024]{1,0:T(8,128)(2,1)} async-done(((bf16[4096,1024]{1,0:T(8,128)(2,1)}), bf16[512,1024]{1,0:T(8,128)(2,1)}) %reduce-scatter.14.cloned.1.call-update) | async-done | bytes 1048592 | tf_op jit(solution)/shard_map/reduce_scatter | solution.py:95
  1331.2 28.2 %all-gather.20.cloned.1.call-done = bf16[1536,1024]{1,0:T(8,128)(2,1)} async-done(((bf16[384,1024]{1,0:T(8,128)(2,1)}), bf16[1536,1024]{1,0:T(8,128)(2,1)}) %all-gather.20.cloned.1.call-update) | async-done | bytes 3145744 | tf_op jit(solution)/shard_map/all_gather | solution.py:113
  1359.4 4.2 fusion.69
  1363.6 69.2 %all-reduce.3.cloned.1.call-done = (bf16[32,2048]{1,0:T(8,128)(2,1)}, bf16[128,3072]{1,0:T(8,128)(2,1)}, bf16[128,1024]{1,0:T(8,128)(2,1)}, bf16[128,4096]{1,0:T(8,128)(2,1)}, bf16[512,1024]{1,0:T(8,128)(2,1)}) async-done(((bf16[32,2048]{1,0:T(8,128)(2,1)}, bf16[128,3072]{1,0:T(8,128)(2,1)}, bf16[128,1024]{1,0:T(8,128)(2,1)}, bf16[128,4096]{1,0:T(8,128)(2,1)}, bf16[512,1024]{1,0:T(8,128)(2,1)}), ...) | async-done | bytes 3276816 | tf_op jit(solution)/shard_map/psum | solution.py:98
  (667 shorter events, 289.2 us)
Async XLA Ops:
  7.2 46.0 %all-gather.10.cloned.1.call-start = ((), (), s32[]{:S(2)}) async-start(), calls=%async_computation.9 | async-start | bytes 1179648 | tf_op jit(solution)/shard_map/all_gather | solution.py:71
  7.9 144.8 %all-gather.12.cloned.1.call-start = ((), (), s32[]{:S(2)}) async-start(), calls=%async_computation.10 | async-start | bytes 7077888 | tf_op jit(solution)/shard_map/all_gather | solution.py:71
  8.7 274.9 %all-gather.22.cloned.1.call-start = ((), (), s32[]{:S(2)}) async-start(), calls=%async_computation.20 | async-start | bytes 3932160 | tf_op jit(solution)/shard_map/all_gather | solution.py:113
  9.4 287.7 %all-gather.14.cloned.1.call-start = ((), (), s32[]{:S(2)}) async-start(), calls=%async_computation.11 | async-start | bytes 2359296 | tf_op jit(solution)/shard_map/all_gather | solution.py:71
  10.0 352.6 %all-gather.16.cloned.1.call-start = ((), (), s32[]{:S(2)}) async-start(), calls=%async_computation.12 | async-start | bytes 9437184 | tf_op jit(solution)/shard_map/all_gather | solution.py:71
  10.6 44.0 %copy-start.39 = (s32[384]{0:T(512)}, s32[384]{0:T(512)S(1)}, u32[]{:S(2)}) copy-start(s32[384]{0:T(512)S(1)} %reduce.4) | copy-start | bytes 4612
  10.8 195.0 %copy-start.53 = (s32[3,1]{0,1:T(1,128)}, s32[3,1]{0,1:T(1,128)S(1)}, u32[]{:S(2)}) copy-start(s32[3,1]{0,1:T(1,128)S(1)} %reduce-window.4) | copy-start | bytes 40
  10.9 194.9 %copy-start.55 = (s32[3]{0:T(128)}, s32[3]{0:T(128)S(1)}, u32[]{:S(2)}) copy-start(s32[3]{0:T(128)S(1)} %fusion.87) | copy-start | bytes 40
  11.1 45.0 %copy-start.43 = (f32[384]{0:T(512)}, f32[384]{0:T(512)S(1)}, u32[]{:S(2)}) copy-start(f32[384]{0:T(512)S(1)} %broadcast_multiply_fusion.1) | copy-start | bytes 4612
  11.5 41.7 %copy-start.45 = (f32[384]{0:T(512)}, f32[384]{0:T(512)S(1)}, u32[]{:S(2)}) copy-start(f32[384]{0:T(512)S(1)} %fusion.62) | copy-start | bytes 4612
  11.6 43.0 %copy-start.49 = (bf16[3,128]{1,0:T(4,128)(2,1)}, bf16[3,128]{1,0:T(4,128)(2,1)S(1)}, u32[]{:S(2)}) copy-start(bf16[3,128]{1,0:T(4,128)(2,1)S(1)} %get-tuple-element.551) | copy-start | bytes 2308
  11.6 43.0 %copy-start.51 = (bf16[3,128]{1,0:T(4,128)(2,1)}, bf16[3,128]{1,0:T(4,128)(2,1)S(1)}, u32[]{:S(2)}) copy-start(bf16[3,128]{1,0:T(4,128)(2,1)S(1)} %get-tuple-element.552) | copy-start | bytes 2308
  11.7 46.5 %copy-start.47 = (f32[384]{0:T(512)}, f32[384]{0:T(512)S(1)}, u32[]{:S(2)}) copy-start(f32[384]{0:T(512)S(1)} %fusion.84) | copy-start | bytes 4612
  58.2 99.3 %copy-start.32 = (bf16[384,1024]{1,0:T(8,128)(2,1)}, bf16[384,1024]{1,0:T(8,128)(2,1)S(1)}, u32[]{:S(2)}) copy-start(bf16[384,1024]{1,0:T(8,128)(2,1)S(1)} %fusion.61) | copy-start | bytes 2359300
  170.3 36.2 %all-to-all-start = ((bf16[384,3,4,256]{0,3,1,2:T(8,128)(2,1)}), bf16[384,3,4,256]{0,3,1,2:T(8,128)(2,1)S(1)}, u32[]{:S(2)}, u32[]{:S(2)}) async-start(bf16[384,3,4,256]{0,3,1,2:T(8,128)(2,1)} %copy.73), calls=%async_computation | async-start | bytes 4718592 | tf_op jit(solution)/shard_map/all_to_all | solution.py:103
  173.9 313.3 %all-gather.18.cloned.1.call-start = ((), (), s32[]{:S(2)}) async-start(), calls=%async_computation.13 | async-start | bytes 9437184 | tf_op jit(solution)/shard_map/all_gather | solution.py:71
  278.6 5.0 copy-start.40
  279.9 15.2 %all-to-all-start.1 = ((bf16[4,2,49152]{2,1,0:T(2,128)(2,1)}), bf16[4,2,49152]{2,1,0:T(2,128)(2,1)S(1)}, u32[]{:S(2)}, u32[]{:S(2)}) async-start(bf16[4,2,49152]{2,1,0:T(2,128)(2,1)} %reshape.383), calls=%async_computation.1 | async-start | bytes 1572864 | tf_op jit(solution)/shard_map/all_to_all | solution.py:107
  487.2 10.8 copy-start.11
  487.2 10.8 copy-start.58
  505.2 9.1 copy-start.15
  507.1 6.6 copy-start.37
  507.1 6.6 copy-start.42
  507.1 7.2 copy-start.19
  510.1 15.1 %all-to-all-start.2 = ((bf16[384,1,4,256]{3,0,1,2:T(8,128)(2,1)}), bf16[384,1,4,256]{3,0,1,2:T(8,128)(2,1)S(1)}, u32[]{:S(2)}, u32[]{:S(2)}) async-start(bf16[384,1,4,256]{3,0,1,2:T(8,128)(2,1)} %copy.78), calls=%async_computation.2 | async-start | bytes 1572864 | tf_op jit(solution)/shard_map/all_to_all | solution.py:103
  513.6 372.4 %reduce-scatter.10.cloned.1.call-start = ((), (), s32[]{:S(2)}) async-start(), calls=%async_computation.17 | async-start | bytes 2359296 | tf_op jit(solution)/shard_map/reduce_scatter | solution.py:95
  516.9 391.7 %reduce-scatter.6.cloned.1.call-start = ((), (), s32[]{:S(2)}) async-start(), calls=%async_computation.15 | async-start | bytes 1179648 | tf_op jit(solution)/shard_map/reduce_scatter | solution.py:95
  525.7 10.0 copy-start.17
  547.2 4.5 copy-start.5
  563.3 4.5 copy-start.5
  579.4 4.5 copy-start.5
  583.9 4.9 copy-start.3
  583.9 4.9 copy-start.30
  583.9 5.8 copy-start.18
  589.7 10.0 copy-start.17
  611.2 4.5 copy-start.5
  627.2 4.5 copy-start.5
  647.8 4.9 copy-start.3
  647.8 4.9 copy-start.30
  647.8 5.8 copy-start.18
  653.6 10.0 copy-start.17
  675.1 4.5 copy-start.5
  707.2 4.5 copy-start.5
  711.7 4.9 copy-start.3
  711.7 4.9 copy-start.30
  711.7 5.8 copy-start.18
  717.5 10.0 copy-start.17
  755.0 4.5 copy-start.5
  771.1 4.5 copy-start.5
  775.6 4.9 copy-start.3
  775.6 4.9 copy-start.30
  775.6 5.8 copy-start.18
  835.0 6.7 copy-start.46
  835.0 6.7 copy-start.14
  835.0 6.7 copy-start.48
  846.8 182.5 %reduce-scatter.8.cloned.1.call-start = ((), (), s32[]{:S(2)}) async-start(), calls=%async_computation.16 | async-start | bytes 7077888 | tf_op jit(solution)/shard_map/reduce_scatter | solution.py:95
  852.5 327.0 %reduce-scatter.12.cloned.1.call-start = ((), (), s32[]{:S(2)}) async-start(), calls=%async_computation.18 | async-start | bytes 9437184 | tf_op jit(solution)/shard_map/reduce_scatter | solution.py:95
  862.2 467.5 %reduce-scatter.14.cloned.1.call-start = ((), (), s32[]{:S(2)}) async-start(), calls=%async_computation.19 | async-start | bytes 9437184 | tf_op jit(solution)/shard_map/reduce_scatter | solution.py:95
  874.4 485.0 %all-gather.20.cloned.1.call-start = ((), (), s32[]{:S(2)}) async-start(), calls=%async_computation.14 | async-start | bytes 3932160 | tf_op jit(solution)/shard_map/all_gather | solution.py:113
  885.9 443.9 %copy-start.16 = (f32[384,1024]{1,0:T(8,128)S(1)}, f32[384,1024]{1,0:T(8,128)}, u32[]{:S(2)}) copy-start(f32[384,1024]{1,0:T(8,128)} %copy-done.15) | copy-start | bytes 4718596
  885.9 443.9 %copy-start.21 = (f32[384,1024]{1,0:T(8,128)S(1)}, f32[384,1024]{1,0:T(8,128)}, u32[]{:S(2)}) copy-start(f32[384,1024]{1,0:T(8,128)} %get-tuple-element.519) | copy-start | bytes 4718596
  885.9 546.9 %all-reduce.3.cloned.1.call-start = ((), (), s32[]{:S(2)}) async-start(), calls=%async_computation.21 | async-start | bytes 6553600 | tf_op jit(solution)/shard_map/psum | solution.py:98
  1329.8 29.6 %copy-start.38 = (s32[1536]{0:T(1024)S(1)}, s32[1536]{0:T(1024)}, u32[]{:S(2)}) copy-start(s32[1536]{0:T(1024)} %copy-done.36) | copy-start | bytes 18436
  1432.8 5.0 copy-start.29
  (84 other events, 191.5 us)
Sparse Core Ops, SparseCore 0:
  10.1 42.9 all-gather.9
  55.4 97.3 all-gather.11
  154.4 29.1 all-gather.21
  185.5 51.9 all-gather.13
  239.5 123.0 all-gather.15
  364.5 122.6 all-gather.17
  518.5 67.2 reduce-scatter.9
  847.0 61.6 reduce-scatter.5
  912.2 117.0 reduce-scatter.7
  1032.8 146.6 reduce-scatter.11
  1183.1 146.5 reduce-scatter.13
  1331.7 27.6 all-gather.19
  1362.1 70.6 all-reduce.2
where the time goes:
time: 1460 us; the launch traced here: 1450 us
  waiting for transfers between devices  871 us (60%)
  matrix products  213 us (15%)
  local copies, waits for them, and re-layouts  174 us (12%)
  blocking collectives  71 us (5%)
  other arithmetic  65.3 us (4%)
  loops' own time  27.9 us (2%)
  between operations  14.8 us (1%)
    reduce_scatter x5, waiting for transfers between devices, weight_grad(): lax.psum_scatter(term().astype(jnp.bfloat16), 'fsdp', scatter_dimension=0...  444 us
    all_gather x5, waiting for transfers between devices, weight_rows(): lax.all_gather(weight, 'fsdp', axis=0, tiled=True)  310 us
    dot_general x28, matrix products, contract_rows(): lax.dot_general(left, right, (((0,), (0,)), ((), ())), preferred_element_...  78.2 us
    dot_general x40, matrix products, contract_cols(): lax.dot_general(left, right, (((1,), (1,)), ((), ())), preferred_element_...  74.3 us
    psum x1, waiting for transfers between devices, weight_grad(): shard = lax.psum(shard.astype(jnp.bfloat16), 'seq').astype(jnp.float32)  69.2 us
    dynamic_update_slice x24, local copies, waits for them, and re-layouts, head_backward(): lax.scan(step, (zeros, zeros), jnp.arange(group // block))  45.4 us
    all_to_all x1, blocking collectives, to_rows(): lax.all_to_all(packed, 'seq', split_axis=0, concat_axis=2, tiled=True)  39.8 us
    all_gather x1, blocking collectives, on_device(): order_all = lax.all_gather(places, 'seq', axis=0, tiled=True)  31.2 us
  transfers between devices with their start and end apart: 16, of which 12 were waited for; matrix products, arithmetic and copies ran while one was open for 28% of the time, Pallas kernels for 0%

commit v1 on v0

--- a/solution.py
+++ b/solution.py
@@ -13,6 +13,27 @@
 NEG = -1e30
 BASE = 10000.0
 BLOCK_ROWS = 512
+
+
+def in_order(blocks, dim):
+    blocks = jnp.moveaxis(blocks, 0, dim)
+    lengths = blocks.shape
+    return blocks.reshape(*lengths[:dim], lengths[dim] * lengths[dim + 1], *lengths[dim + 2 :])
+
+
+def grow_blocks(x, axis):
+    devices, place = (lax.axis_size(axis), lax.axis_index(axis))
+    parts, stride = (x[None], 1)
+    while stride < devices:
+        other = lax.ppermute(parts, axis, [(i, i ^ stride) for i in range(devices)])
+        low = place & stride == 0
+        parts = jnp.concatenate([jnp.where(low, parts, other), jnp.where(low, other, parts)])
+        stride *= 2
+    return parts
+
+
+def gather_by_bits(value, axis, dim):
+    return in_order(grow_blocks(value, axis), dim)
 
 
 def time_embedding(steps):
@@ -66,11 +87,7 @@
 
 def weight_rows(left, weight):
     return (
-        jnp.dot(
-            left,
-            lax.all_gather(weight, "fsdp", axis=0, tiled=True),
-            preferred_element_type=jnp.float32,
-        ),
+        jnp.dot(left, gather_by_bits(weight, "fsdp", 0), preferred_element_type=jnp.float32),
         weight,
     )
 

time: 1460 us -> 2000 us (1.37)
  waiting for transfers between devices: 871 us -> 1270 us
  local copies, waits for them, and re-layouts: 174 us -> 246 us
  other arithmetic: 65.3 us -> 103 us
  matrix products: 213 us -> 248 us
  blocking collectives: 71 us -> 44.8 us
    ppermute x0 -> x15, waiting for transfers between devices: none -> 948 us  [grow_blocks(): other = lax.ppermute(parts, axis, [(i, i ^ stride) for i in range(devices)])]
    all_gather x5 -> x4, waiting for transfers between devices: 310 us -> 0.04 us  [weight_cols(): lax.all_gather(weight, 'fsdp', axis=0, tiled=True)]
    reduce_scatter x5, waiting for transfers between devices: 444 us -> 191 us  [weight_grad(): lax.psum_scatter(term().astype(jnp.bfloat16), 'fsdp', scatter_dimension=0...]
    all_gather x1, blocking collectives: 31.2 us -> 5.16 us  [on_device(): order_all = lax.all_gather(places, 'seq', axis=0, tiled=True)]
    concatenate x0 -> x15, other arithmetic: none -> 25.3 us  [grow_blocks(): jnp.concatenate([jnp.where(low, parts, other), jnp.where(low, other, part...]
    dot_general x40, matrix products: 74.3 us -> 97 us  [contract_cols(): lax.dot_general(left, right, (((1,), (1,)), ((), ())), preferred_element_...]
  transfers between devices with their start and end apart: 16 -> 30, of which waited for: 12 -> 17; matrix products, arithmetic and copies ran while one was open for 28% -> 28% of each run, Pallas kernels for 0% -> 0%
where the time goes in v1:
time: 2000 us; the launch traced here: 1980 us
  waiting for transfers between devices  1270 us (64%)
  matrix products  248 us (12%)
  local copies, waits for them, and re-layouts  246 us (12%)
  other arithmetic  103 us (5%)
  blocking collectives  44.8 us (2%)
  loops' own time  30 us (2%)
  starting transfers between devices  29.6 us (1%)
    ppermute x15, waiting for transfers between devices, grow_blocks(): other = lax.ppermute(parts, axis, [(i, i ^ stride) for i in range(devices)])  948 us
    reduce_scatter x5, waiting for transfers between devices, weight_grad(): lax.psum_scatter(term().astype(jnp.bfloat16), 'fsdp', scatter_dimension=0...  191 us
    dot_general x40, matrix products, contract_cols(): lax.dot_general(left, right, (((1,), (1,)), ((), ())), preferred_element_...  97 us
    dot_general x28, matrix products, contract_rows(): lax.dot_general(left, right, (((0,), (0,)), ((), ())), preferred_element_...  86.2 us
    psum x1, waiting for transfers between devices, weight_grad(): shard = lax.psum(shard.astype(jnp.bfloat16), 'seq').astype(jnp.float32)  67.7 us
    dynamic_update_slice x24, local copies, waits for them, and re-layouts, head_backward(): lax.scan(step, (zeros, zeros), jnp.arange(group // block))  53.2 us
  transfers between devices with their start and end apart: 30, of which 17 were waited for; matrix products, arithmetic and copies ran while one was open for 28% of the time, Pallas kernels for 0%

profile of v1, /device:TPU:0, one launch (start us, length us, event | category | flops | bytes accessed | tf_op | source)
XLA Modules:
  0.0 1983.1 jit_solution(4169073583891785016)
XLA Ops:
  17.7 5.2 all-gather
  23.6 37.5 %collective-permute-done = bf16[1,32,2048]{2,1,0:T(8,128)(2,1)S(1)} collective-permute-done((bf16[1,32,2048]{2,1,0:T(8,128)(2,1)S(1)}, bf16[1,32,2048]{2,1,0:T(8,128)(2,1)S(1)}, u32[]{:S(2)}, u32[]{:S(2)}) %collective-permute-start) | collective-permute-done | bytes 131104 | tf_op jit(solution)/shard_map/ppermute | solution.py:28
  65.0 6.3 collective-permute-done.6
  73.9 82.9 %collective-permute-done.1 = bf16[2,32,2048]{2,1,0:T(8,128)(2,1)S(1)} collective-permute-done((bf16[2,32,2048]{2,1,0:T(8,128)(2,1)S(1)}, bf16[2,32,2048]{2,1,0:T(8,128)(2,1)S(1)}, u32[]{:S(2)}, u32[]{:S(2)}) %collective-permute-start.1) | collective-permute-done | bytes 262176 | tf_op jit(solution)/shard_map/ppermute | solution.py:28
  157.1 31.6 %collective-permute-done.7 = bf16[2,128,1024]{2,1,0:T(8,128)(2,1)S(1)} collective-permute-done((bf16[2,128,1024]{2,1,0:T(8,128)(2,1)S(1)}, bf16[2,128,1024]{2,1,0:T(8,128)(2,1)S(1)}, u32[]{:S(2)}, u32[]{:S(2)}) %collective-permute-start.7) | collective-permute-done | bytes 524320 | tf_op jit(solution)/shard_map/ppermute | solution.py:28
  192.5 33.4 %collective-permute-done.2 = bf16[4,32,2048]{2,1,0:T(8,128)(2,1)S(1)} collective-permute-done((bf16[4,32,2048]{2,1,0:T(8,128)(2,1)S(1)}, bf16[4,32,2048]{2,1,0:T(8,128)(2,1)S(1)}, u32[]{:S(2)}, u32[]{:S(2)}) %collective-permute-start.2) | collective-permute-done | bytes 524320 | tf_op jit(solution)/shard_map/ppermute | solution.py:28
  234.0 3.5 collective-permute-start.10
  237.6 96.0 %collective-permute-done.8 = bf16[4,128,1024]{2,1,0:T(8,128)(2,1)S(1)} collective-permute-done((bf16[4,128,1024]{2,1,0:T(8,128)(2,1)S(1)}, bf16[4,128,1024]{2,1,0:T(8,128)(2,1)S(1)}, u32[]{:S(2)}, u32[]{:S(2)}) %collective-permute-start.8) | collective-permute-done | bytes 1048608 | tf_op jit(solution)/shard_map/ppermute | solution.py:28
  335.2 162.9 %collective-permute-done.5 = bf16[4,128,3072]{2,1,0:T(8,128)(2,1)S(1)} collective-permute-done((bf16[4,128,3072]{2,1,0:T(8,128)(2,1)S(1)}, bf16[4,128,3072]{2,1,0:T(8,128)(2,1)S(1)}, u32[]{:S(2)}, u32[]{:S(2)}) %collective-permute-start.5) | collective-permute-done | bytes 3145760 | tf_op jit(solution)/shard_map/ppermute | solution.py:28
  501.7 4.7 fusion.97
  521.5 4.7 all-to-all-start
  531.3 4.5 fusion.49
  535.8 18.9 all-to-all-done
  559.6 133.9 %while.88 = (s32[]{:T(128)}, bf16[4,1536,64]{1,2,0:T(8,128)(2,1)}, f32[4,1536]{1,0:T(4,128)}, s32[4]{0:T(128)}, bf16[1536,256]{1,0:T(8,128)(2,1)}, /*index=5*/bf...) while((s32[]{:T(128)}, bf16[4,1536,64]{1,2,0:T(8,128)(2,1)}, ...), condition=%wide.region_10.11_spmd, body=%wide.region_5.10_spmd.sunk | while | flops 208436736 | bytes 12641802 | solution.py:227
  565.9 23.0 %while.91 = (s32[]{:T(128)}, bf16[3,512,64]{1,2,0:T(8,128)(2,1)}, f32[3,512]{1,0:T(4,128)}, s32[3]{0:T(128)}, s32[1536]{0:T(1024)S(1)}, /*index=5*/bf16[1536,64]...) while((s32[]{:T(128)}, bf16[3,512,64]{1,2,0:T(8,128)(2,1)}, ...), condition=%wide.region_9.9_spmd, body=%wide.region_6.8_spmd.sunk | while | flops 208436736 | bytes 10257083 | solution.py:155
  599.4 23.0 %while.91 = (s32[]{:T(128)}, bf16[3,512,64]{1,2,0:T(8,128)(2,1)}, f32[3,512]{1,0:T(4,128)}, s32[3]{0:T(128)}, s32[1536]{0:T(1024)S(1)}, /*index=5*/bf16[1536,64]...) while((s32[]{:T(128)}, bf16[3,512,64]{1,2,0:T(8,128)(2,1)}, ...), condition=%wide.region_9.9_spmd, body=%wide.region_6.8_spmd.sunk | while | flops 208436736 | bytes 10257083 | solution.py:155
  632.9 23.0 %while.91 = (s32[]{:T(128)}, bf16[3,512,64]{1,2,0:T(8,128)(2,1)}, f32[3,512]{1,0:T(4,128)}, s32[3]{0:T(128)}, s32[1536]{0:T(1024)S(1)}, /*index=5*/bf16[1536,64]...) while((s32[]{:T(128)}, bf16[3,512,64]{1,2,0:T(8,128)(2,1)}, ...), condition=%wide.region_9.9_spmd, body=%wide.region_6.8_spmd.sunk | while | flops 208436736 | bytes 10257083 | solution.py:155
  666.4 23.0 %while.91 = (s32[]{:T(128)}, bf16[3,512,64]{1,2,0:T(8,128)(2,1)}, f32[3,512]{1,0:T(4,128)}, s32[3]{0:T(128)}, s32[1536]{0:T(1024)S(1)}, /*index=5*/bf16[1536,64]...) while((s32[]{:T(128)}, bf16[3,512,64]{1,2,0:T(8,128)(2,1)}, ...), condition=%wide.region_9.9_spmd, body=%wide.region_6.8_spmd.sunk | while | flops 208436736 | bytes 10257083 | solution.py:155
  699.7 3.7 all-to-all-start.1
  703.4 97.8 %collective-permute-done.11 = bf16[4,128,4096]{2,1,0:T(8,128)(2,1)} collective-permute-done((bf16[4,128,4096]{2,1,0:T(8,128)(2,1)}, bf16[4,128,4096]{2,1,0:T(8,128)(2,1)}, u32[]{:S(2)}, u32[]{:S(2)}) %collective-permute-start.11) | collective-permute-done | bytes 4194336 | tf_op jit(solution)/shard_map/ppermute | solution.py:28
  801.2 5.4 broadcast_select_fusion.3
  806.5 7.5 pad_maximum_fusion
  821.4 8.7 fusion.98
  830.1 12.0 fusion.44
  842.1 8.5 multiply_reduce_fusion.1
  852.7 4.0 convolution_convert_fusion.5
  859.8 3.5 all-to-all-start.2
  866.6 8.2 all-to-all-done.2
  875.4 280.9 %while.90 = (s32[]{:T(128)}, bf16[4,1536,64]{1,2,0:T(8,128)(2,1)}, bf16[4,1536,64]{1,2,0:T(8,128)(2,1)}, bf16[4,1536,64]{1,2,0:T(8,128)(2,1)}, s32[4]{0:T(128)},...) while((s32[]{:T(128)}, bf16[4,1536,64]{1,2,0:T(8,128)(2,1)}, ...), condition=%wide.region_20.21_spmd, body=%wide.region_16.20_spmd.sunk | while | flops 513375776 | bytes 51172928 | solution.py:269
  886.7 52.4 %while.92 = (s32[]{:T(128)}, f32[1536,64]{0,1:T(8,128)}, f32[1536,64]{0,1:T(8,128)}, f32[3,512,64]{1,0,2:T(4,128)}, s32[3]{0:T(128)}, /*index=5*/s32[1536]{0:T(1...) while((s32[]{:T(128)}, f32[1536,64]{0,1:T(8,128)}, ...), condition=%wide.region_19.19_spmd.clone, body=%wide.region_17.18_spmd.clone.sunk | while | flops 511704576 | bytes 33446152 | solution.py:182
  895.6 3.6 dynamic_update_slice.65
  912.9 3.6 dynamic_update_slice.65
  930.5 3.6 dynamic_update_slice.65
  956.9 52.3 %while.92 = (s32[]{:T(128)}, f32[1536,64]{0,1:T(8,128)}, f32[1536,64]{0,1:T(8,128)}, f32[3,512,64]{1,0,2:T(4,128)}, s32[3]{0:T(128)}, /*index=5*/s32[1536]{0:T(1...) while((s32[]{:T(128)}, f32[1536,64]{0,1:T(8,128)}, ...), condition=%wide.region_19.19_spmd.clone, body=%wide.region_17.18_spmd.clone.sunk | while | flops 511704576 | bytes 33446152 | solution.py:182
  965.8 3.6 dynamic_update_slice.65
  983.1 3.6 dynamic_update_slice.65
  1000.6 3.6 dynamic_update_slice.65
  1027.1 52.3 %while.92 = (s32[]{:T(128)}, f32[1536,64]{0,1:T(8,128)}, f32[1536,64]{0,1:T(8,128)}, f32[3,512,64]{1,0,2:T(4,128)}, s32[3]{0:T(128)}, /*index=5*/s32[1536]{0:T(1...) while((s32[]{:T(128)}, f32[1536,64]{0,1:T(8,128)}, ...), condition=%wide.region_19.19_spmd.clone, body=%wide.region_17.18_spmd.clone.sunk | while | flops 511704576 | bytes 33446152 | solution.py:182
  1036.0 3.6 dynamic_update_slice.65
  1053.3 3.6 dynamic_update_slice.65
  1070.8 3.6 dynamic_update_slice.65
  1097.3 52.3 %while.92 = (s32[]{:T(128)}, f32[1536,64]{0,1:T(8,128)}, f32[1536,64]{0,1:T(8,128)}, f32[3,512,64]{1,0,2:T(4,128)}, s32[3]{0:T(128)}, /*index=5*/s32[1536]{0:T(1...) while((s32[]{:T(128)}, f32[1536,64]{0,1:T(8,128)}, ...), condition=%wide.region_19.19_spmd.clone, body=%wide.region_17.18_spmd.clone.sunk | while | flops 511704576 | bytes 33446152 | solution.py:182
  1106.2 3.6 dynamic_update_slice.65
  1123.4 3.6 dynamic_update_slice.65
  1141.0 3.6 dynamic_update_slice.65
  1156.4 3.3 pad_maximum_fusion.7
  1159.7 4.3 copy.79
  1163.9 39.6 %all_to_all.63 = bf16[1536,3,1,256]{3,1,2,0:T(4,128)(2,1)S(1)} all-to-all(bf16[1536,3,1,256]{3,1,2,0:T(4,128)(2,1)S(1)} %copy.79), channel_id=1, replica_groups=mesh['seq'=4,'fsdp'=8] {'seq'}, dimensions={0} | all-to-all | bytes 4718592 | tf_op jit(solution)/shard_map/all_to_all | solution.py:124
  1205.3 4.4 copy.81
  1209.8 6.7 fusion.63
  1221.7 10.6 convolution_convert_fusion
  1234.1 5.4 convolution_convert_fusion.2
  1240.7 8.9 convolution_convert_fusion.1
  1252.3 26.2 %collective-permute-done.12 = bf16[1,512,1024]{2,1,0:T(8,128)(2,1)S(1)} collective-permute-done((bf16[1,512,1024]{2,1,0:T(8,128)(2,1)S(1)}, bf16[1,512,1024]{2,1,0:T(8,128)(2,1)S(1)}, u32[]{:S(2)}, u32[]{:S(2)}) %collective-permute-start.12) | collective-permute-done | bytes 1048608 | tf_op jit(solution)/shard_map/ppermute | solution.py:28
  1278.9 106.3 %collective-permute-done.13 = bf16[2,512,1024]{2,1,0:T(8,128)(2,1)S(1)} collective-permute-done((bf16[2,512,1024]{2,1,0:T(8,128)(2,1)S(1)}, bf16[2,512,1024]{2,1,0:T(8,128)(2,1)S(1)}, u32[]{:S(2)}, u32[]{:S(2)}) %collective-permute-start.13) | collective-permute-done | bytes 2097184 | tf_op jit(solution)/shard_map/ppermute | solution.py:28
  1385.9 266.9 %collective-permute-done.14 = bf16[4,512,1024]{2,1,0:T(8,128)(2,1)S(1)} collective-permute-done((bf16[4,512,1024]{2,1,0:T(8,128)(2,1)S(1)}, bf16[4,512,1024]{2,1,0:T(8,128)(2,1)S(1)}, u32[]{:S(2)}, u32[]{:S(2)}) %collective-permute-start.14) | collective-permute-done | bytes 4194336 | tf_op jit(solution)/shard_map/ppermute | solution.py:28
  1652.8 3.7 broadcast_select_fusion.1
  1656.5 7.7 pad_maximum_fusion.1
  1664.2 10.3 add_convert_fusion
  1674.7 40.6 %reduce-scatter.8.cloned.1.call-done = bf16[128,3072]{1,0:T(8,128)(2,1)} async-done(((bf16[1024,3072]{1,0:T(8,128)(2,1)}), bf16[128,3072]{1,0:T(8,128)(2,1)}) %reduce-scatter.8.cloned.1.call-update) | async-done | bytes 786448 | tf_op jit(solution)/shard_map/reduce_scatter | solution.py:112
  1715.3 150.2 %reduce-scatter.12.cloned.1.call-done = bf16[128,4096]{1,0:T(8,128)(2,1)} async-done(((bf16[1024,4096]{1,0:T(8,128)(2,1)}), bf16[128,4096]{1,0:T(8,128)(2,1)}) %reduce-scatter.12.cloned.1.call-update) | async-done | bytes 1048592 | tf_op jit(solution)/shard_map/reduce_scatter | solution.py:112
  1865.5 29.7 %all-gather.9.cloned.1.call-done = bf16[1536,1024]{1,0:T(8,128)(2,1)} async-done(((bf16[384,1024]{1,0:T(8,128)(2,1)}), bf16[1536,1024]{1,0:T(8,128)(2,1)}) %all-gather.9.cloned.1.call-update) | async-done | bytes 3145744 | tf_op jit(solution)/shard_map/all_gather | solution.py:130
  1895.2 4.2 fusion.69
  1900.8 67.7 %all-reduce.3.cloned.1.call-done = (bf16[32,2048]{1,0:T(8,128)(2,1)}, bf16[128,3072]{1,0:T(8,128)(2,1)}, bf16[128,1024]{1,0:T(8,128)(2,1)}, bf16[128,4096]{1,0:T(8,128)(2,1)}, bf16[512,1024]{1,0:T(8,128)(2,1)}) async-done(((bf16[32,2048]{1,0:T(8,128)(2,1)}, bf16[128,3072]{1,0:T(8,128)(2,1)}, bf16[128,1024]{1,0:T(8,128)(2,1)}, bf16[128,4096]{1,0:T(8,128)(2,1)}, bf16[512,1024]{1,0:T(8,128)(2,1)}), ...) | async-done | bytes 3276816 | tf_op jit(solution)/shard_map/psum | solution.py:115
  (626 shorter events, 445.8 us)
Async XLA Ops:
  7.2 8.1 copy-start.58
  7.2 8.1 copy-start.57
  7.2 8.1 copy-start.59
  7.2 8.3 copy-start.7
  7.2 524.1 %all-gather.19.cloned.1.call-start = ((), (), s32[]{:S(2)}) async-start(), calls=%async_computation.19 | async-start | bytes 3932160 | tf_op jit(solution)/shard_map/all_gather | solution.py:130
  8.0 822.1 %all-gather.11.cloned.1.call-start = ((), (), s32[]{:S(2)}) async-start(), calls=%async_computation.10 | async-start | bytes 9437184 | tf_op jit(solution)/shard_map/all_gather | solution.py:96
  8.7 833.4 %all-gather.13.cloned.1.call-start = ((), (), s32[]{:S(2)}) async-start(), calls=%async_computation.11 | async-start | bytes 9437184 | tf_op jit(solution)/shard_map/all_gather | solution.py:96
  9.4 843.3 %all-gather.15.cloned.1.call-start = ((), (), s32[]{:S(2)}) async-start(), calls=%async_computation.12 | async-start | bytes 2359296 | tf_op jit(solution)/shard_map/all_gather | solution.py:96
  10.0 1199.8 %all-gather.17.cloned.1.call-start = ((), (), s32[]{:S(2)}) async-start(), calls=%async_computation.13 | async-start | bytes 7077888 | tf_op jit(solution)/shard_map/all_gather | solution.py:96
  10.1 220.8 %collective-permute-start.9 = (bf16[1,128,4096]{2,1,0:T(8,128)(2,1)}, bf16[1,128,4096]{2,1,0:T(8,128)(2,1)}, u32[]{:S(2)}, u32[]{:S(2)}) collective-permute-start(bf16[1,128,4096]{2,1,0:T(8,128)(2,1)} %bitcast.39), channel_id=1, source_target_pairs={{0,1},{1,0},{2,3},{3,2},{4,5},{5,4},{6,7},{7,6},{8,9},{9,8},{10,11... | collective-permute-start | bytes 3145736 | tf_op jit(solution)/shard_map/ppermute | solution.py:28
  13.1 48.0 %collective-permute-start.3 = (bf16[1,128,3072]{2,1,0:T(8,128)(2,1)S(1)}, bf16[1,128,3072]{2,1,0:T(8,128)(2,1)}, u32[]{:S(2)}, u32[]{:S(2)}) collective-permute-start(bf16[1,128,3072]{2,1,0:T(8,128)(2,1)S(1)} %bitcast.226), channel_id=1, source_target_pairs={{0,1},{1,0},{2,3},{3,2},{4,5},{5,4},{6,7},{7,6},{8,9},{9,8},{10,11... | collective-permute-start | bytes 2359304 | tf_op jit(solution)/shard_map/ppermute | solution.py:28
  13.2 47.9 %collective-permute-start = (bf16[1,32,2048]{2,1,0:T(8,128)(2,1)S(1)}, bf16[1,32,2048]{2,1,0:T(8,128)(2,1)S(1)}, u32[]{:S(2)}, u32[]{:S(2)}) collective-permute-start(bf16[1,32,2048]{2,1,0:T(8,128)(2,1)S(1)} %bitcast.235), channel_id=1, source_target_pairs={{0,1},{1,0},{2,3},{3,2},{4,5},{5,4},{6,7},{7,6},{8,9},{9,8},{10,11... | collective-permute-start | bytes 393224 | tf_op jit(solution)/shard_map/ppermute | solution.py:28
  15.1 56.1 %collective-permute-start.6 = (bf16[1,128,1024]{2,1,0:T(8,128)(2,1)}, bf16[1,128,1024]{2,1,0:T(8,128)(2,1)}, u32[]{:S(2)}, u32[]{:S(2)}) collective-permute-start(bf16[1,128,1024]{2,1,0:T(8,128)(2,1)} %bitcast.37), channel_id=1, source_target_pairs={{0,1},{1,0},{2,3},{3,2},{4,5},{5,4},{6,7},{7,6},{8,9},{9,8},{10,11... | collective-permute-start | bytes 786440 | tf_op jit(solution)/shard_map/ppermute | solution.py:28
  15.3 516.0 %copy-start.38 = (s32[384]{0:T(512)}, s32[384]{0:T(512)S(1)}, u32[]{:S(2)}) copy-start(s32[384]{0:T(512)S(1)} %reduce.4) | copy-start | bytes 4612
  15.5 47.1 %copy-start.51 = (s32[3,1]{0,1:T(1,128)}, s32[3,1]{0,1:T(1,128)S(1)}, u32[]{:S(2)}) copy-start(s32[3,1]{0,1:T(1,128)S(1)} %reduce-window.4) | copy-start | bytes 40
  15.5 47.1 %copy-start.54 = (s32[3]{0:T(128)}, s32[3]{0:T(128)S(1)}, u32[]{:S(2)}) copy-start(s32[3]{0:T(128)S(1)} %fusion.87) | copy-start | bytes 40
  15.7 212.1 %copy-start.41 = (f32[384]{0:T(512)}, f32[384]{0:T(512)S(1)}, u32[]{:S(2)}) copy-start(f32[384]{0:T(512)S(1)} %broadcast_multiply_fusion.1) | copy-start | bytes 4612
  16.1 7.5 copy-start.43
  22.9 39.9 %copy-start.35 = (s32[1536]{0:T(1024)}, s32[1536]{0:T(1024)S(1)}, u32[]{:S(2)}) copy-start(s32[1536]{0:T(1024)S(1)} %reduce.3) | copy-start | bytes 18436
  62.8 126.2 %collective-permute-start.4 = (bf16[2,128,3072]{2,1,0:T(8,128)(2,1)S(1)}, bf16[2,128,3072]{2,1,0:T(8,128)(2,1)S(1)}, u32[]{:S(2)}, u32[]{:S(2)}) collective-permute-start(bf16[2,128,3072]{2,1,0:T(8,128)(2,1)S(1)} %pad_maximum_fusion.11), channel_id=1, source_target_pairs={{0,2},{1,3},{2,0},{3,1},{4,6},{5,7},{6,4},{7,5},{8,10},{9,11},{10,... | collective-permute-start | bytes 4718600 | tf_op jit(solution)/shard_map/ppermute | solution.py:28
  64.3 92.6 %collective-permute-start.1 = (bf16[2,32,2048]{2,1,0:T(8,128)(2,1)S(1)}, bf16[2,32,2048]{2,1,0:T(8,128)(2,1)S(1)}, u32[]{:S(2)}, u32[]{:S(2)}) collective-permute-start(bf16[2,32,2048]{2,1,0:T(8,128)(2,1)S(1)} %pad_maximum_fusion.18), channel_id=1, source_target_pairs={{0,2},{1,3},{2,0},{3,1},{4,6},{5,7},{6,4},{7,5},{8,10},{9,11},{10,... | collective-permute-start | bytes 786440 | tf_op jit(solution)/shard_map/ppermute | solution.py:28
  72.4 116.3 %collective-permute-start.7 = (bf16[2,128,1024]{2,1,0:T(8,128)(2,1)S(1)}, bf16[2,128,1024]{2,1,0:T(8,128)(2,1)S(1)}, u32[]{:S(2)}, u32[]{:S(2)}) collective-permute-start(bf16[2,128,1024]{2,1,0:T(8,128)(2,1)S(1)} %pad_maximum_fusion.17), channel_id=1, source_target_pairs={{0,2},{1,3},{2,0},{3,1},{4,6},{5,7},{6,4},{7,5},{8,10},{9,11},{10,... | collective-permute-start | bytes 1572872 | tf_op jit(solution)/shard_map/ppermute | solution.py:28
  157.0 68.9 %collective-permute-start.2 = (bf16[4,32,2048]{2,1,0:T(8,128)(2,1)S(1)}, bf16[4,32,2048]{2,1,0:T(8,128)(2,1)S(1)}, u32[]{:S(2)}, u32[]{:S(2)}) collective-permute-start(bf16[4,32,2048]{2,1,0:T(8,128)(2,1)S(1)} %pad_maximum_fusion.16), channel_id=1, source_target_pairs={{0,4},{1,5},{2,6},{3,7},{4,0},{5,1},{6,2},{7,3},{8,12},{9,13},{10,... | collective-permute-start | bytes 1572872 | tf_op jit(solution)/shard_map/ppermute | solution.py:28
  188.9 144.7 %collective-permute-start.8 = (bf16[4,128,1024]{2,1,0:T(8,128)(2,1)S(1)}, bf16[4,128,1024]{2,1,0:T(8,128)(2,1)S(1)}, u32[]{:S(2)}, u32[]{:S(2)}) collective-permute-start(bf16[4,128,1024]{2,1,0:T(8,128)(2,1)S(1)} %pad_maximum_fusion.13), channel_id=1, source_target_pairs={{0,4},{1,5},{2,6},{3,7},{4,0},{5,1},{6,2},{7,3},{8,12},{9,13},{10,... | collective-permute-start | bytes 3145736 | tf_op jit(solution)/shard_map/ppermute | solution.py:28
  189.5 36.6 %copy-start.47 = (bf16[3,128]{1,0:T(4,128)(2,1)S(1)}, bf16[3,128]{1,0:T(4,128)(2,1)}, u32[]{:S(2)}) copy-start(bf16[3,128]{1,0:T(4,128)(2,1)} %get-tuple-element.581) | copy-start | bytes 2308
  189.5 36.6 %copy-start.49 = (bf16[3,128]{1,0:T(4,128)(2,1)S(1)}, bf16[3,128]{1,0:T(4,128)(2,1)}, u32[]{:S(2)}) copy-start(bf16[3,128]{1,0:T(4,128)(2,1)} %get-tuple-element.582) | copy-start | bytes 2308
  189.5 36.8 %copy-start.52 = (s32[3,1]{0,1:T(1,128)S(1)}, s32[3,1]{0,1:T(1,128)}, u32[]{:S(2)}) copy-start(s32[3,1]{0,1:T(1,128)} %copy-done.51) | copy-start | bytes 40
  189.5 36.8 %copy-start.55 = (s32[3]{0:T(128)S(1)}, s32[3]{0:T(128)}, u32[]{:S(2)}) copy-start(s32[3]{0:T(128)} %copy-done.54) | copy-start | bytes 40
  189.5 308.6 %collective-permute-start.5 = (bf16[4,128,3072]{2,1,0:T(8,128)(2,1)S(1)}, bf16[4,128,3072]{2,1,0:T(8,128)(2,1)S(1)}, u32[]{:S(2)}, u32[]{:S(2)}) collective-permute-start(bf16[4,128,3072]{2,1,0:T(8,128)(2,1)S(1)} %pad_maximum_fusion.5), channel_id=1, source_target_pairs={{0,4},{1,5},{2,6},{3,7},{4,0},{5,1},{6,2},{7,3},{8,12},{9,13},{10,... | collective-permute-start | bytes 9437192 | tf_op jit(solution)/shard_map/ppermute | solution.py:28
  234.0 292.1 %collective-permute-start.10 = (bf16[2,128,4096]{2,1,0:T(8,128)(2,1)}, bf16[2,128,4096]{2,1,0:T(8,128)(2,1)}, u32[]{:S(2)}, u32[]{:S(2)}) collective-permute-start(bf16[2,128,4096]{2,1,0:T(8,128)(2,1)} %pad_maximum_fusion.9), channel_id=1, source_target_pairs={{0,2},{1,3},{2,0},{3,1},{4,6},{5,7},{6,4},{7,5},{8,10},{9,11},{10,... | collective-permute-start | bytes 6291464 | tf_op jit(solution)/shard_map/ppermute | solution.py:28
  521.5 33.2 %all-to-all-start = ((bf16[384,3,4,256]{0,3,1,2:T(8,128)(2,1)}), bf16[384,3,4,256]{0,3,1,2:T(8,128)(2,1)}, u32[]{:S(2)}, u32[]{:S(2)}) async-start(bf16[384,3,4,256]{0,3,1,2:T(8,128)(2,1)} %copy.73), calls=%async_computation | async-start | bytes 4718592 | tf_op jit(solution)/shard_map/all_to_all | solution.py:120
  531.3 269.8 %collective-permute-start.11 = (bf16[4,128,4096]{2,1,0:T(8,128)(2,1)}, bf16[4,128,4096]{2,1,0:T(8,128)(2,1)}, u32[]{:S(2)}, u32[]{:S(2)}) collective-permute-start(bf16[4,128,4096]{2,1,0:T(8,128)(2,1)} %pad_maximum_fusion.3), channel_id=1, source_target_pairs={{0,4},{1,5},{2,6},{3,7},{4,0},{5,1},{6,2},{7,3},{8,12},{9,13},{10,... | collective-permute-start | bytes 12582920 | tf_op jit(solution)/shard_map/ppermute | solution.py:28
  696.5 104.6 %copy-start.10 = (bf16[2,128,4096]{2,1,0:T(8,128)(2,1)S(1)}, bf16[2,128,4096]{2,1,0:T(8,128)(2,1)}, u32[]{:S(2)}) copy-start(bf16[2,128,4096]{2,1,0:T(8,128)(2,1)} %copy-done.9) | copy-start | bytes 6291460
  699.7 114.4 %all-to-all-start.1 = ((bf16[4,2,49152]{2,1,0:T(2,128)(2,1)}), bf16[4,2,49152]{2,1,0:T(2,128)(2,1)S(1)}, u32[]{:S(2)}, u32[]{:S(2)}) async-start(bf16[4,2,49152]{2,1,0:T(2,128)(2,1)} %reshape.403), calls=%async_computation.1 | async-start | bytes 1572864 | tf_op jit(solution)/shard_map/all_to_all | solution.py:124
  842.1 8.5 copy-start.5
  852.7 11.3 copy-start.12
  856.8 6.6 copy-start.40
  856.8 7.2 copy-start.16
  859.8 15.1 all-to-all-start.2
  863.3 811.4 %reduce-scatter.10.cloned.1.call-start = ((), (), s32[]{:S(2)}) async-start(), calls=%async_computation.16 | async-start | bytes 2359296 | tf_op jit(solution)/shard_map/reduce_scatter | solution.py:112
  866.6 808.1 %reduce-scatter.6.cloned.1.call-start = ((), (), s32[]{:S(2)}) async-start(), calls=%async_computation.14 | async-start | bytes 1179648 | tf_op jit(solution)/shard_map/reduce_scatter | solution.py:112
  875.6 11.1 copy-start.14
  939.1 6.8 copy-start.15
  945.9 11.1 copy-start.14
  1009.2 6.8 copy-start.15
  1016.0 11.1 copy-start.14
  1079.4 6.8 copy-start.15
  1086.2 11.1 copy-start.14
  1149.6 6.8 copy-start.15
  1209.8 6.7 copy-start.44
  1209.8 6.7 copy-start.8
  1209.8 6.7 copy-start.46
  1221.6 453.1 %reduce-scatter.14.cloned.1.call-start = ((), (), s32[]{:S(2)}) async-start(), calls=%async_computation.18 | async-start | bytes 9437184 | tf_op jit(solution)/shard_map/reduce_scatter | solution.py:112
  1232.3 483.0 %reduce-scatter.8.cloned.1.call-start = ((), (), s32[]{:S(2)}) async-start(), calls=%async_computation.15 | async-start | bytes 7077888 | tf_op jit(solution)/shard_map/reduce_scatter | solution.py:112
  1239.5 625.9 %reduce-scatter.12.cloned.1.call-start = ((), (), s32[]{:S(2)}) async-start(), calls=%async_computation.17 | async-start | bytes 9437184 | tf_op jit(solution)/shard_map/reduce_scatter | solution.py:112
  1249.5 645.7 %all-gather.9.cloned.1.call-start = ((), (), s32[]{:S(2)}) async-start(), calls=%async_computation.9 | async-start | bytes 3932160 | tf_op jit(solution)/shard_map/all_gather | solution.py:130
  1250.8 27.7 %collective-permute-start.12 = (bf16[1,512,1024]{2,1,0:T(8,128)(2,1)S(1)}, bf16[1,512,1024]{2,1,0:T(8,128)(2,1)S(1)}, u32[]{:S(2)}, u32[]{:S(2)}) collective-permute-start(bf16[1,512,1024]{2,1,0:T(8,128)(2,1)S(1)} %bitcast.220), channel_id=1, source_target_pairs={{0,1},{1,0},{2,3},{3,2},{4,5},{5,4},{6,7},{7,6},{8,9},{9,8},{10,11... | collective-permute-start | bytes 3145736 | tf_op jit(solution)/shard_map/ppermute | solution.py:28
  1278.8 106.4 %collective-permute-start.13 = (bf16[2,512,1024]{2,1,0:T(8,128)(2,1)S(1)}, bf16[2,512,1024]{2,1,0:T(8,128)(2,1)S(1)}, u32[]{:S(2)}, u32[]{:S(2)}) collective-permute-start(bf16[2,512,1024]{2,1,0:T(8,128)(2,1)S(1)} %pad_maximum_fusion.10), channel_id=1, source_target_pairs={{0,2},{1,3},{2,0},{3,1},{4,6},{5,7},{6,4},{7,5},{8,10},{9,11},{10,... | collective-permute-start | bytes 6291464 | tf_op jit(solution)/shard_map/ppermute | solution.py:28
  1385.8 267.0 %collective-permute-start.14 = (bf16[4,512,1024]{2,1,0:T(8,128)(2,1)S(1)}, bf16[4,512,1024]{2,1,0:T(8,128)(2,1)S(1)}, u32[]{:S(2)}, u32[]{:S(2)}) collective-permute-start(bf16[4,512,1024]{2,1,0:T(8,128)(2,1)S(1)} %pad_maximum_fusion.4), channel_id=1, source_target_pairs={{0,4},{1,5},{2,6},{3,7},{4,0},{5,1},{6,2},{7,3},{8,12},{9,13},{10,... | collective-permute-start | bytes 12582920 | tf_op jit(solution)/shard_map/ppermute | solution.py:28
  1656.5 7.7 copy-start.6
  1674.5 220.7 %copy-start.37 = (s32[1536]{0:T(1024)S(1)}, s32[1536]{0:T(1024)}, u32[]{:S(2)}) copy-start(s32[1536]{0:T(1024)} %copy-done.35) | copy-start | bytes 18436
  1674.6 293.9 %all-reduce.3.cloned.1.call-start = ((), (), s32[]{:S(2)}) async-start(), calls=%async_computation.20 | async-start | bytes 6553600 | tf_op jit(solution)/shard_map/psum | solution.py:115
  1865.5 34.0 %copy-start.13 = (f32[384,1024]{1,0:T(8,128)S(1)}, f32[384,1024]{1,0:T(8,128)}, u32[]{:S(2)}) copy-start(f32[384,1024]{1,0:T(8,128)} %copy-done.12) | copy-start | bytes 4718596
  1865.5 34.0 %copy-start.18 = (f32[384,1024]{1,0:T(8,128)S(1)}, f32[384,1024]{1,0:T(8,128)}, u32[]{:S(2)}) copy-start(f32[384,1024]{1,0:T(8,128)} %get-tuple-element.519) | copy-start | bytes 4718596
  (49 other events, 114.6 us)
Sparse Core Ops, SparseCore 0:
  9.6 31.2 all-gather.18
  43.0 271.2 all-gather.10
  316.5 180.1 all-gather.12
  498.7 141.0 all-gather.14
  641.8 133.0 all-gather.16
  867.9 67.6 reduce-scatter.9
  1221.7 63.4 reduce-scatter.5
  1288.8 282.6 reduce-scatter.13
  1575.1 140.1 reduce-scatter.7
  1718.7 146.6 reduce-scatter.11
  1867.6 27.6 all-gather.8
  1897.8 70.6 all-reduce.2
